TPU v7x, 512 devices: a whole 4x8x8 slice. The times are simulated.
512 devices in a mesh: blk: 64 (over z_hi, x, y), grp: 8 (over z_lo, core).
Axes of the slice: x: 4, y: 8, z: 8 (z_hi: 2, z_lo: 4; z = z_hi * 4 + z_lo), core: 2. Of those that a mesh axis runs over, the one named last changes fastest.
Arguments:
- orbitals: bfloat16 [512, 64, 4096], P(('blk', 'grp')), may hold values from -6 to 6
- offsets: int32 [512, 3], replicated, may hold values from 0 to 15
- pair_list: int32 [512, 3], replicated, may hold values 0 or 1
Outputs:
- exchange_action: float32 [512, 64, 4096], P(('blk', 'grp'))
All inputs are finite; a program needn't handle non-finite values.
Results may differ from a plain program's by a relative error of at most 0.0015.
Values may be sent and summed in bfloat16 or wider, within the bound.
No kernel may reach another device: no remote copies, remote signals or barrier semaphores. Data moves between devices by JAX's collectives and lax.ppermute only.
A program may use at most 128 MiB of HBM per device.

v0:
```python
import jax
import jax.numpy as jnp
import numpy as np
from jax import lax
from jax.experimental import pallas as pl
from jax.experimental.pallas import tpu as pltpu
from jax.sharding import PartitionSpec as P


B = 64
PITCH = 65
AXES = ("blk", "grp")


def constants():
    level = np.arange(1, B + 1, dtype=np.float64)
    sines = np.sqrt(2.0 / (B + 1)) * np.sin(np.pi * level[:, None] * level[None, :] / (B + 1))
    eigen = 2.0 - 2.0 * np.cos(np.pi * level / (B + 1))
    pair = eigen[:, None] + np.tile(eigen, 2)[None, :] + 0.5
    return [np.asarray(t, np.float32) for t in (np.pad(sines, ((0, 0), (32, 32))), pair, np.tile(eigen[:, None], (1, 128)))]


SEXT, LEV, LA = constants()
bf16, f32 = jnp.bfloat16, jnp.float32
OUT = pltpu.VMEM


def split(x):
    hi = x.astype(bf16)
    lo = (x - hi.astype(f32)).astype(bf16)
    return hi, lo


def dot(a, b):
    return jnp.dot(a, b, preferred_element_type=f32)


def iota(shape, dim):
    return lax.broadcasted_iota(jnp.int32, shape, dim)


def shifted_pair(sext, g0, g1):
    lane = iota((B, 128), 1)
    r0 = pltpu.roll(sext, (96 - g0) % 128, 1)
    r1 = pltpu.roll(sext, (160 - g1) % 128, 1)
    return jnp.concatenate([jnp.where(lane < B, r0, 0.0), jnp.where(lane >= B, r1, 0.0)], 0)


def lhs_quad(wide):
    lane = iota((128, 128), 1)
    both = wide + pltpu.roll(wide, 64, 1)
    hi, lo = split(both)
    return jnp.concatenate([hi, lo], 1)


def lhs_halves(wide):
    lane = iota((B, 128), 1)
    block = jnp.where(lane < B, wide[:B], 0.0)
    low = jnp.where(lane < 32, block, 0.0)
    high = pltpu.roll(jnp.where(lane >= 32, block, 0.0), 96, 1)
    both = jnp.concatenate([low, high], 0)
    both = both + pltpu.roll(both, 32, 1)
    hi, lo = split(both)
    whole = (hi.astype(f32) + pltpu.roll(lo.astype(f32), 64, 1)).astype(bf16)
    return jnp.concatenate([whole, jnp.zeros_like(whole)], 1)


def halves_through(lhs, x):
    hi, lo = split(x)
    z = dot(lhs, jnp.concatenate([hi, lo, hi, lo], 0))
    out = []
    lane = iota((32, 128), 1)
    for k in range(x.shape[1] // 128):
        v = z[:, 128 * k:128 * k + 128]
        straight = jnp.where(lane < B, v[:32], v[96:])
        out.append(straight + pltpu.roll(jnp.where(lane < B, v[32:64], v[64:96]), 64, 1))
    return jnp.concatenate(out, 1)


def row_quad(wide):
    hi, lo = split(wide)
    top = jnp.concatenate([hi, lo], 1)
    bottom = jnp.concatenate([hi, jnp.zeros_like(lo)], 1)
    return jnp.concatenate([top, bottom], 0)


def rows_through(x, w):
    hi, lo = split(x)
    z = dot(jnp.concatenate([hi, lo], 1), w)
    return z[:, :128] + z[:, 128:]


def cols_through(lhs, x):
    hi, lo = split(x)
    z = dot(lhs, jnp.concatenate([hi, lo, hi, lo], 0))
    if z.shape[0] == B:
        return z
    lane = iota((B, x.shape[1]), 1)
    return jnp.where(lane % 128 < B, z[:B], z[B:])


def neighbour(tab, nbr):
    count = lax.axis_size(AXES)
    here = lax.axis_index(AXES)
    if not nbr:
        return [0, 0, 0], 0, f32(1.0 if nbr == 0 else 0.0)
    step = jnp.where(here % 2 == 0, nbr, -nbr)
    there = lax.rem(here + step + count, count)
    gaps = [tab[d, here] - tab[d, there] for d in range(3)]
    up = step > 0
    weight = tab[2 + abs(nbr), jnp.where(up, there, here)].astype(f32)
    return gaps, jnp.where(up, 1, 0), weight


ROWS = 1408


def prepare_kernel(calls, tab, sext_ref, *outs):
    sext = sext_ref[...]
    for call, nbrs in enumerate(calls):
        m, steps = outs[2 * call], outs[2 * call + 1]
        lone = nbrs[1] is None
        info = [neighbour(tab, n) for n in (nbrs[:1] * 2 if lone else nbrs)]
        ga, gb, gc = [[i[0][d] for i in info] for d in range(3)]
        role = [i[1] for i in info]
        w = [i[2] for i in info]
        ma = shifted_pair(sext, role[0] * ga[0], role[1] * ga[1])
        m[0:128] = lhs_quad(ma)
        m[128:256] = lhs_quad(ma.T)
        mb = shifted_pair(sext, role[0] * gb[0], role[1] * gb[1])
        m[256:384] = lhs_halves(mb) if lone else lhs_quad(mb)
        m[384:512] = lhs_halves(mb.T) if lone else lhs_quad(mb.T)
        mc = shifted_pair(sext, role[0] * gc[0], role[1] * gc[1])
        m[512:768] = row_quad(mc.T)
        weight = jnp.where(iota((128, 128), 1) < B, w[0], w[1])
        m[768:1024] = row_quad(-mc * weight)
        ii, nn = iota((128, 256), 0), iota((128, 256), 1)
        row, col = iota((B, 256), 0), iota((B, 256), 1)
        for s in range(2):
            hit = ((nn // 64) % 2 == s) & (ii // 64 == nn // 128) & (ii % 64 == nn % 64 + gc[s])
            m[1024 + 128 * s:1152 + 128 * s] = jnp.where(hit, 1.0, 0.0).astype(bf16)
            m[1280 + B * s:1344 + B * s] = jnp.where(col == row + ga[s], 1.0, 0.0).astype(bf16)
            steps[s] = jnp.full((8, 128), gb[s], jnp.int32)


def prepare(tab, calls):
    vm = pl.BlockSpec(memory_space=pltpu.VMEM)
    outs = []
    for _ in calls:
        outs += [OUT((ROWS, 256), bf16), OUT((2, 8, 128), jnp.int32)]
    return pl.pallas_call(
        lambda *refs: prepare_kernel(calls, *refs),
        out_shape=outs, in_specs=[pl.BlockSpec(memory_space=pltpu.SMEM), vm], out_specs=[vm] * len(outs),
        cost_estimate=pl.CostEstimate(flops=3_000_000_000, bytes_accessed=1 << 20, transcendentals=0),
        compiler_params=pltpu.CompilerParams(vmem_limit_bytes=16 << 20),
    )(tab, jnp.asarray(SEXT))


def pair_kernel(TB, TA, first, last, lone, x_hbm, n0_ref, n1_ref, acc_ref, m, steps, lev_ref, la_ref, out_ref,
                x_ref, stage_ref, sems, xp0, xp1, y_ref, z_ref):
    load = pltpu.make_async_copy(x_hbm, x_ref, sems.at[0])
    load.start()
    if first:
        load.wait()
        n0_ref = x_ref
    gb = [jnp.max(steps[s]) for s in range(2)]
    lane = iota((B, 128), 1)
    for s, (n_ref, xp) in enumerate(((n0_ref, xp0), (n1_ref, xp1))[:1 if lone else 2]):
        xp[:, :1024] = jnp.zeros((B, 1024), bf16)
        xp[:, 5120:] = jnp.zeros((B, 1024), bf16)
        odd = gb[s] & 1
        keep = lane < jnp.where(odd == 1, B, 2 * B)
        before = jnp.zeros((B, 128), f32)
        for i in range(4):
            v = dot(m[1280 + B * s:1344 + B * s, :B], n_ref[:, 1024 * i:1024 * i + 1024])
            for j in range(8):
                col = pltpu.roll(v[:, 128 * j:128 * j + 128], 64 * odd, 1)
                at = 1024 * i + 128 * j + 896
                xp[:, at:at + 128] = jnp.where(keep, before, col).astype(bf16)
                before = col
        xp[:, 4992:5120] = jnp.where(keep, before, 0.0).astype(bf16)
    if not first:
        load.wait()
    q0, q1 = 8 + (gb[0] >> 1), 8 + (gb[1] >> 1)
    if lone:
        q1, xp1 = q0 + 16, xp0
    pairs = 16 if lone else 32

    for t in range(pairs // TB):
        wins, even, odds = [], [], []
        for j in range(TB):
            bp = t * TB + j
            l0 = pl.multiple_of((bp + q0) * 128, 128)
            l1 = pl.multiple_of((bp + q1) * 128, 128)
            wins.append(jnp.concatenate([xp0[:, pl.ds(l0, 128)], xp1[:, pl.ds(l1, 128)]], 1))
            v = x_ref[:, 128 * bp:128 * bp + 128].astype(f32)
            u = x_ref[:, 128 * bp + 2048:128 * bp + 2176].astype(f32) if lone else v
            r = pltpu.roll(v, 64, 1)
            even.append(jnp.where(lane < B, v, pltpu.roll(u, 64, 1) if lone else r))
            odds.append(jnp.where(lane < B, r, u))
        y = dot(jnp.concatenate(wins, 0), m[1024:1280])
        for j in range(TB):
            for o in range(2):
                y_ref[t * 2 * TB + 2 * j + o] = y[64 * j:64 * j + 64, 128 * o:128 * o + 128].astype(bf16)
        d = jnp.concatenate([y[:, :128], y[:, 128:]], 0) * jnp.concatenate(even + odds, 0)
        d = rows_through(d, m[512:768])
        d = jnp.concatenate([d[64 * (o * TB + j):64 * (o * TB + j) + 64] for j in range(TB) for o in range(2)], 1)
        d = cols_through(m[0:B if lone else 128], d)
        for k in range(2 * TB):
            at = (t * 2 * TB + k) * PITCH
            z_ref[at:at + 64, :] = d[:, 128 * k:128 * k + 128]

    lev = lev_ref[...]
    if lone:
        lev = jnp.where(iota((32, 128), 1) < B, lev[:32], lev[32:])
    deep = 32 if lone else 64
    through = (lambda a, d: halves_through(m[a:a + 128, :128], d)) if lone else (lambda a, d: cols_through(m[a:a + 128], d))
    for t in range(64 // TA):
        parts = [z_ref[pl.ds(t * TA + k, deep, stride=PITCH), :] for k in range(TA)]
        d = through(256, jnp.concatenate(parts, 1))
        g = jnp.concatenate([1.0 / (lev + la_ref[t * TA + k:t * TA + k + 1, :]) for k in range(TA)], 1)
        d = through(384, d * g)
        for k in range(TA):
            z_ref[pl.ds(t * TA + k, deep, stride=PITCH), :] = d[:, 128 * k:128 * k + 128]

    stores = []
    target = stage_ref if last else out_ref
    for t in range(pairs // TB):
        parts = [z_ref[(t * 2 * TB + k) * PITCH:(t * 2 * TB + k) * PITCH + 64, :] for k in range(2 * TB)]
        d = cols_through(m[128:192 if lone else 256], jnp.concatenate(parts, 1))
        d = jnp.concatenate([d[:, 128 * k:128 * k + 128] for k in range(2 * TB)], 0)
        d = rows_through(d, m[768:1024])
        for j in range(TB):
            v = [d[64 * k:64 * k + 64] * y_ref[t * 2 * TB + k].astype(f32) for k in (2 * j, 2 * j + 1)]
            at = (t * TB + j) * 128
            if lone:
                low = jnp.where(lane < B, v[0], pltpu.roll(v[1], 64, 1))
                high = jnp.where(lane < B, pltpu.roll(v[0], 64, 1), v[1])
                target[:, at:at + 128] = acc_ref[:, at:at + 128] + low
                target[:, at + 2048:at + 2176] = acc_ref[:, at + 2048:at + 2176] + high
            else:
                r = jnp.where(lane < B, v[0], v[1]) + pltpu.roll(jnp.where(lane < B, v[1], v[0]), 64, 1)
                target[:, at:at + 128] = r if first else acc_ref[:, at:at + 128] + r
        if last:
            for at in (t * TB * 128, t * TB * 128 + 2048)[:2 if lone else 1]:
                part = pl.ds(at, TB * 128)
                stores.append(pltpu.make_async_copy(stage_ref.at[:, part], out_ref.at[:, part], sems.at[1 + len(stores)]))
                stores[-1].start()
    for store in stores:
        store.wait()


def pair_call(made, x, n0, n1, acc, last=False, TB=16, TA=32):
    first, lone = acc is None, n1 is None
    TB = min(TB, 8) if lone else TB
    vm = pl.BlockSpec(memory_space=pltpu.VMEM)
    hbm = pl.BlockSpec(memory_space=pl.ANY)
    args = [x] + ([] if first else [n0]) + ([] if lone else [n1]) + ([] if first else [acc])
    args += [*made, jnp.asarray(LEV), jnp.asarray(LA)]
    specs = [hbm] + [vm] * (len(args) - 1)

    def body(*refs):
        refs = list(refs)
        if first:
            refs.insert(1, None)
        if lone:
            refs.insert(2, refs[1])
        if first:
            refs.insert(3, None)
        pair_kernel(TB, TA, first, last, lone, *refs)
    return pl.pallas_call(
        body,
        out_shape=jax.ShapeDtypeStruct((B, B * B), f32) if last else OUT((B, B * B), f32),
        in_specs=specs, out_specs=hbm if last else vm,
        scratch_shapes=[
            pltpu.VMEM((B, B * B), bf16), pltpu.VMEM((B, B * B) if last else (8, 128), f32),
            pltpu.SemaphoreType.DMA((1 + 32 // TB,)),
            pltpu.VMEM((B, 6144), bf16), pltpu.VMEM((B, 6144), bf16),
            pltpu.VMEM((B, B, 128), bf16), pltpu.VMEM((B * PITCH + 8, 128), f32),
        ],
        cost_estimate=pl.CostEstimate(flops=10_000_000_000, bytes_accessed=4 << 20, transcendentals=0),
        compiler_params=pltpu.CompilerParams(vmem_limit_bytes=32 << 20),
    )(*args)


def permute(value, target):
    count = lax.axis_size(AXES)
    return lax.ppermute(value, AXES, [(p, target(p) % count) for p in range(count)])


def per_device(orbitals, offsets, pair_list):
    x = orbitals.reshape(B, B * B)
    tab = jnp.concatenate([offsets.T, pair_list.T], 0)
    swap = lambda p: p ^ 1
    near = permute(x, lambda p: p + 2 if p % 2 else p - 2)
    own = permute(x, swap)
    made = prepare(tab, ((0, 1), (2, -1), (-2, 3), (-3, None)))
    later, mine = lax.optimization_barrier((x, made[0]))
    back = permute(later, lambda p: p - 2 if p % 2 else p + 2)
    acc = pair_call([mine, made[1]], x, x, own, None)
    near, acc = lax.optimization_barrier((near, acc))
    near_swap = permute(near, swap)
    far = permute(near, lambda p: p + 1 if p % 2 else p - 1)
    acc = pair_call(made[2:4], x, near, near_swap, acc)
    back_swap = permute(back, swap)
    acc = pair_call(made[4:6], x, back, back_swap, acc)
    acc = pair_call(made[6:8], x, far, None, acc, last=True)
    return acc.reshape(orbitals.shape)


def solution(mesh):
    in_specs = (P(AXES, None, None), P(), P())
    return jax.shard_map(
        per_device, mesh=mesh, in_specs=in_specs, out_specs=P(AXES, None, None), check_vma=False
    )
```

profile of v0, /device:TPU:1, one launch (start us, length us, event | category | flops | bytes accessed | tf_op | source)
XLA Modules:
  0.0 67.2 jit_solution(6672658937203027843)
XLA Ops:
  0.0 0.0 copy-start.3
  0.0 8.9 %collective-permute-start.1 = (bf16[64,4096]{1,0:T(8,128)(2,1)}, bf16[64,4096]{1,0:T(8,128)(2,1)S(1)}, u32[]{:S(2)}, u32[]{:S(2)}) collective-permute-start(bf16[64,4096]{1,0:T(8,128)(2,1)} %bitcast.4), channel_id=1, source_target_pairs={{0,1},{1,0},{2,3},{3,2},{4,5},{5,4},{6,7},{7,6},{8,9},{9,8},{10,11... | collective-permute-start | bytes 1572872 | tf_op jit(solution)/shard_map/ppermute | solution.py:288
  8.9 1.9 %collective-permute-start = (bf16[64,4096]{1,0:T(8,128)(2,1)}, bf16[64,4096]{1,0:T(8,128)(2,1)S(1)}, u32[]{:S(2)}, u32[]{:S(2)}) collective-permute-start(bf16[64,4096]{1,0:T(8,128)(2,1)} %bitcast.5), channel_id=1, source_target_pairs={{0,510},{1,3},{2,0},{3,5},{4,2},{5,7},{6,4},{7,9},{8,6},{9,11},{10... | collective-permute-start | bytes 1572872 | tf_op jit(solution)/shard_map/ppermute | solution.py:288
  10.8 0.7 %pad_add_fusion.refs_0_ = s32[6,512]{1,0:T(8,128)S(1)} fusion(s32[3,512]{1,0:T(4,128)} %bitcast.11, s32[3,512]{1,0:T(4,128)} %bitcast.12), kind=kLoop, calls=%fused_computation | loop fusion | flops 3072 | bytes 24576 | tf_op jit(solution)/shard_map/concatenate | solution.py:293
  11.5 0.0 copy-done.3
  11.5 0.0 copy-start
  11.5 0.0 copy-start.1
  11.6 0.0 copy-start.2
  11.6 2.3 %shard_map.64 = (bf16[1408,256]{1,0:T(8,128)(2,1)S(1)}, s32[2,8,128]{2,1,0:T(8,128)S(1)}, bf16[1408,256]{1,0:T(8,128)(2,1)S(1)}, s32[2,8,128]{2,1,0:T(8,128)S(1)...) custom-call(s32[6,512]{1,0:T(8,128)S(1)} %pad_add_fusion.refs_0_, ...), custom_call_target="tpu_custom_call" | custom-call | flops 3000000000 | bytes 1048576 | tf_op jit(solution)/shard_map/pallas_call | solution.py:151
  13.9 0.0 copy-done
  13.9 10.4 %collective-permute-start.3 = (bf16[64,4096]{1,0:T(8,128)(2,1)S(1)}, bf16[64,4096]{1,0:T(8,128)(2,1)S(1)}, u32[]{:S(2)}, u32[]{:S(2)}) collective-permute-start(bf16[64,4096]{1,0:T(8,128)(2,1)S(1)} %bitcast.6), channel_id=1, source_target_pairs={{0,2},{1,511},{2,4},{3,1},{4,6},{5,3},{6,8},{7,5},{8,10},{9,7},{10... | collective-permute-start | bytes 1572872 | tf_op jit(solution)/shard_map/ppermute | solution.py:288
  24.3 0.0 collective-permute-done.1.refs_1_
  24.3 0.0 copy-done.1
  24.3 0.0 copy-done.2
  24.4 5.9 %shard_map.65.refs_3_ = f32[64,4096]{1,0:T(8,128)S(1)} custom-call(bf16[64,4096]{1,0:T(8,128)(2,1)S(1)} %bitcast.7, bf16[64,4096]{1,0:T(8,128)(2,1)S(1)} %collective-permute-done.1.refs_1_, bf16[1408,256]{1,0:T(8,128)(2,1)S(1)} %get-tuple-element.18.refs_2_, s32[2,8,128]{2,1,0:T(8,128)S(1)} %get-tuple-element.19.refs_3_, f32[64,128]{1,0:T(8,128)S(1)} %copy-done.2, ...), custom_call_target="tpu_custom_call" | custom-call | flops 10000000000 | bytes 4194304 | tf_op jit(solution)/shard_map/pallas_call | solution.py:271
  30.2 1.3 %collective-permute-done.refs_1_ = bf16[64,4096]{1,0:T(8,128)(2,1)S(1)} collective-permute-done((bf16[64,4096]{1,0:T(8,128)(2,1)}, bf16[64,4096]{1,0:T(8,128)(2,1)S(1)}, u32[]{:S(2)}, u32[]{:S(2)}) %collective-permute-start) | collective-permute-done | bytes 524320 | tf_op jit(solution)/shard_map/ppermute | solution.py:288
  31.5 5.9 %collective-permute-start.5 = (bf16[64,4096]{1,0:T(8,128)(2,1)S(1)}, bf16[64,4096]{1,0:T(8,128)(2,1)S(1)}, u32[]{:S(2)}, u32[]{:S(2)}) collective-permute-start(bf16[64,4096]{1,0:T(8,128)(2,1)S(1)} %collective-permute-done.refs_1_), channel_id=1, source_target_pairs={{0,1},{1,0},{2,3},{3,2},{4,5},{5,4},{6,7},{7,6},{8,9},{9,8},{10,11... | collective-permute-start | bytes 1572872 | tf_op jit(solution)/shard_map/ppermute | solution.py:288
  37.5 1.9 %collective-permute-start.2 = (bf16[64,4096]{1,0:T(8,128)(2,1)S(1)}, bf16[64,4096]{1,0:T(8,128)(2,1)S(1)}, u32[]{:S(2)}, u32[]{:S(2)}) collective-permute-start(bf16[64,4096]{1,0:T(8,128)(2,1)S(1)} %collective-permute-done.refs_1_), channel_id=1, source_target_pairs={{0,511},{1,2},{2,1},{3,4},{4,3},{5,6},{6,5},{7,8},{8,7},{9,10},{10... | collective-permute-start | bytes 1572872 | tf_op jit(solution)/shard_map/ppermute | solution.py:288
  39.4 0.0 collective-permute-done.3.refs_1_
  39.4 10.1 %collective-permute-start.4 = (bf16[64,4096]{1,0:T(8,128)(2,1)S(1)}, bf16[64,4096]{1,0:T(8,128)(2,1)S(1)}, u32[]{:S(2)}, u32[]{:S(2)}) collective-permute-start(bf16[64,4096]{1,0:T(8,128)(2,1)S(1)} %collective-permute-done.3.refs_1_), channel_id=1, source_target_pairs={{0,1},{1,0},{2,3},{3,2},{4,5},{5,4},{6,7},{7,6},{8,9},{9,8},{10,11... | collective-permute-start | bytes 1572872 | tf_op jit(solution)/shard_map/ppermute | solution.py:288
  49.5 0.0 collective-permute-done.5.refs_2_
  49.6 6.1 %shard_map.66.refs_3_ = f32[64,4096]{1,0:T(8,128)S(1)} custom-call(bf16[64,4096]{1,0:T(8,128)(2,1)S(1)} %bitcast.8, bf16[64,4096]{1,0:T(8,128)(2,1)S(1)} %collective-permute-done.refs_1_, bf16[64,4096]{1,0:T(8,128)(2,1)S(1)} %collective-permute-done.5.refs_2_, f32[64,4096]{1,0:T(8,128)S(1)} %shard_map.65.refs_3_, ...), custom_call_target="tpu_custom_call" | custom-call | flops 10000000000 | bytes 4194304 | tf_op jit(solution)/shard_map/pallas_call | solution.py:271
  55.6 0.0 collective-permute-done.4.refs_2_
  55.6 6.1 %shard_map.67.refs_2_ = f32[64,4096]{1,0:T(8,128)S(1)} custom-call(bf16[64,4096]{1,0:T(8,128)(2,1)S(1)} %bitcast.9, bf16[64,4096]{1,0:T(8,128)(2,1)S(1)} %collective-permute-done.3.refs_1_, bf16[64,4096]{1,0:T(8,128)(2,1)S(1)} %collective-permute-done.4.refs_2_, f32[64,4096]{1,0:T(8,128)S(1)} %shard_map.66.refs_3_, ...), custom_call_target="tpu_custom_call" | custom-call | flops 10000000000 | bytes 4194304 | tf_op jit(solution)/shard_map/pallas_call | solution.py:271
  61.7 0.0 collective-permute-done.2.refs_1_
  61.7 5.3 %shard_map.68 = f32[64,4096]{1,0:T(8,128)} custom-call(bf16[64,4096]{1,0:T(8,128)(2,1)S(1)} %bitcast.10, bf16[64,4096]{1,0:T(8,128)(2,1)S(1)} %collective-permute-done.2.refs_1_, f32[64,4096]{1,0:T(8,128)S(1)} %shard_map.67.refs_2_, bf16[1408,256]{1,0:T(8,128)(2,1)S(1)} %get-tuple-element.27.refs_3_, s32[2,8,128]{2,1,0:T(8,128)S(1)} %get-tuple-element.28.refs_4_, ...), custom_call_target="tpu_custom_call" | custom-call | flops 10000000000 | bytes 4194304 | tf_op jit(solution)/shard_map/pallas_call | solution.py:271
Async XLA Ops:
  0.0 11.5 %copy-start.3 = (f32[64,128]{1,0:T(8,128)S(1)}, f32[64,128]{1,0:T(8,128)}, u32[]{:S(2)}) copy-start(f32[64,128]{1,0:T(8,128)} %constant.6.clone.refs_1_) | copy-start | bytes 98308
  0.0 24.3 %collective-permute-start.1 = (bf16[64,4096]{1,0:T(8,128)(2,1)}, bf16[64,4096]{1,0:T(8,128)(2,1)S(1)}, u32[]{:S(2)}, u32[]{:S(2)}) collective-permute-start(bf16[64,4096]{1,0:T(8,128)(2,1)} %bitcast.4), channel_id=1, source_target_pairs={{0,1},{1,0},{2,3},{3,2},{4,5},{5,4},{6,7},{7,6},{8,9},{9,8},{10,11... | collective-permute-start | bytes 1572872 | tf_op jit(solution)/shard_map/ppermute | solution.py:288
  8.9 22.7 %collective-permute-start = (bf16[64,4096]{1,0:T(8,128)(2,1)}, bf16[64,4096]{1,0:T(8,128)(2,1)S(1)}, u32[]{:S(2)}, u32[]{:S(2)}) collective-permute-start(bf16[64,4096]{1,0:T(8,128)(2,1)} %bitcast.5), channel_id=1, source_target_pairs={{0,510},{1,3},{2,0},{3,5},{4,2},{5,7},{6,4},{7,9},{8,6},{9,11},{10... | collective-permute-start | bytes 1572872 | tf_op jit(solution)/shard_map/ppermute | solution.py:288
  11.5 2.3 %copy-start = (bf16[1,64,4096]{2,1,0:T(8,128)(2,1)S(1)}, bf16[1,64,4096]{2,1,0:T(8,128)(2,1)}, u32[]{:S(2)}) copy-start(bf16[1,64,4096]{2,1,0:T(8,128)(2,1)} %param.6) | copy-start | bytes 1572868
  11.5 12.8 %copy-start.1 = (f32[64,128]{1,0:T(8,128)S(1)}, f32[64,128]{1,0:T(8,128)}, u32[]{:S(2)}) copy-start(f32[64,128]{1,0:T(8,128)} %constant.8.clone.refs_5_.refs_7_.refs_6_) | copy-start | bytes 98308
  11.6 12.8 %copy-start.2 = (f32[64,128]{1,0:T(8,128)S(1)}, f32[64,128]{1,0:T(8,128)}, u32[]{:S(2)}) copy-start(f32[64,128]{1,0:T(8,128)} %constant.7.clone.refs_4_.refs_6_.refs_5_) | copy-start | bytes 98308
  13.9 25.5 %collective-permute-start.3 = (bf16[64,4096]{1,0:T(8,128)(2,1)S(1)}, bf16[64,4096]{1,0:T(8,128)(2,1)S(1)}, u32[]{:S(2)}, u32[]{:S(2)}) collective-permute-start(bf16[64,4096]{1,0:T(8,128)(2,1)S(1)} %bitcast.6), channel_id=1, source_target_pairs={{0,2},{1,511},{2,4},{3,1},{4,6},{5,3},{6,8},{7,5},{8,10},{9,7},{10... | collective-permute-start | bytes 1572872 | tf_op jit(solution)/shard_map/ppermute | solution.py:288
  31.5 18.0 %collective-permute-start.5 = (bf16[64,4096]{1,0:T(8,128)(2,1)S(1)}, bf16[64,4096]{1,0:T(8,128)(2,1)S(1)}, u32[]{:S(2)}, u32[]{:S(2)}) collective-permute-start(bf16[64,4096]{1,0:T(8,128)(2,1)S(1)} %collective-permute-done.refs_1_), channel_id=1, source_target_pairs={{0,1},{1,0},{2,3},{3,2},{4,5},{5,4},{6,7},{7,6},{8,9},{9,8},{10,11... | collective-permute-start | bytes 1572872 | tf_op jit(solution)/shard_map/ppermute | solution.py:288
  37.5 24.2 %collective-permute-start.2 = (bf16[64,4096]{1,0:T(8,128)(2,1)S(1)}, bf16[64,4096]{1,0:T(8,128)(2,1)S(1)}, u32[]{:S(2)}, u32[]{:S(2)}) collective-permute-start(bf16[64,4096]{1,0:T(8,128)(2,1)S(1)} %collective-permute-done.refs_1_), channel_id=1, source_target_pairs={{0,511},{1,2},{2,1},{3,4},{4,3},{5,6},{6,5},{7,8},{8,7},{9,10},{10... | collective-permute-start | bytes 1572872 | tf_op jit(solution)/shard_map/ppermute | solution.py:288
  39.4 16.2 %collective-permute-start.4 = (bf16[64,4096]{1,0:T(8,128)(2,1)S(1)}, bf16[64,4096]{1,0:T(8,128)(2,1)S(1)}, u32[]{:S(2)}, u32[]{:S(2)}) collective-permute-start(bf16[64,4096]{1,0:T(8,128)(2,1)S(1)} %collective-permute-done.3.refs_1_), channel_id=1, source_target_pairs={{0,1},{1,0},{2,3},{3,2},{4,5},{5,4},{6,7},{7,6},{8,9},{9,8},{10,11... | collective-permute-start | bytes 1572872 | tf_op jit(solution)/shard_map/ppermute | solution.py:288
where the time goes:
time: 67.6 us; the launch traced here: 67.2 us
  starting transfers between devices  39.2 us (58%)
  Pallas kernels  25.6 us (38%)
  waiting for transfers between devices  1.32 us (2%)
  other arithmetic  0.72 us (1%)
    ppermute x6, starting transfers between devices, permute(): lax.ppermute(value, AXES, [(p, target(p) % count) for p in range(count)])  39.2 us
    pallas_call x4, Pallas kernels, pair_call(): pl.pallas_call(body, out_shape=jax.ShapeDtypeStruct((B, B * B), f32) if l...  23.3 us
    pallas_call x1, Pallas kernels, prepare(): pl.pallas_call(lambda *refs: prepare_kernel(calls, *refs), out_shape=outs...  2.3 us
  transfers between devices with their start and end apart: 6, of which 1 were waited for; matrix products, arithmetic and copies ran while one was open for 1% of the time, Pallas kernels for 30%

commit v1 on v0

--- a/solution.py
+++ b/solution.py
@@ -92,7 +92,7 @@
 
 def cols_through(lhs, x):
     hi, lo = split(x)
-    z = dot(lhs, jnp.concatenate([hi, lo, hi, lo], 0))
+    z = dot(lhs[:, :192], jnp.concatenate([hi, lo, hi], 0))
     if z.shape[0] == B:
         return z
     lane = iota((B, x.shape[1]), 1)
@@ -154,6 +154,15 @@
         cost_estimate=pl.CostEstimate(flops=3_000_000_000, bytes_accessed=1 << 20, transcendentals=0),
         compiler_params=pltpu.CompilerParams(vmem_limit_bytes=16 << 20),
     )(tab, jnp.asarray(SEXT))
+
+
+def staggered(count, steps):
+    values = {}
+    for i in range(count + 2 * (len(steps) - 1)):
+        for j, step in enumerate(steps):
+            t = i - 2 * j
+            if 0 <= t < count:
+                values[t] = step(t, values.pop(t, None))
 
 
 def pair_kernel(TB, TA, first, last, lone, x_hbm, n0_ref, n1_ref, acc_ref, m, steps, lev_ref, la_ref, out_ref,
@@ -186,48 +195,65 @@
         q1, xp1 = q0 + 16, xp0
     pairs = 16 if lone else 32
 
-    for t in range(pairs // TB):
-        wins, even, odds = [], [], []
+    def moved(t, _):
+        wins = []
         for j in range(TB):
             bp = t * TB + j
             l0 = pl.multiple_of((bp + q0) * 128, 128)
             l1 = pl.multiple_of((bp + q1) * 128, 128)
             wins.append(jnp.concatenate([xp0[:, pl.ds(l0, 128)], xp1[:, pl.ds(l1, 128)]], 1))
+        return dot(jnp.concatenate(wins, 0), m[1024:1280])
+
+    def density(t, y):
+        even, odds = [], []
+        for j in range(TB):
+            bp = t * TB + j
             v = x_ref[:, 128 * bp:128 * bp + 128].astype(f32)
             u = x_ref[:, 128 * bp + 2048:128 * bp + 2176].astype(f32) if lone else v
             r = pltpu.roll(v, 64, 1)
             even.append(jnp.where(lane < B, v, pltpu.roll(u, 64, 1) if lone else r))
             odds.append(jnp.where(lane < B, r, u))
-        y = dot(jnp.concatenate(wins, 0), m[1024:1280])
-        for j in range(TB):
             for o in range(2):
                 y_ref[t * 2 * TB + 2 * j + o] = y[64 * j:64 * j + 64, 128 * o:128 * o + 128].astype(bf16)
         d = jnp.concatenate([y[:, :128], y[:, 128:]], 0) * jnp.concatenate(even + odds, 0)
-        d = rows_through(d, m[512:768])
+        return rows_through(d, m[512:768])
+
+    def first_forward(t, d):
         d = jnp.concatenate([d[64 * (o * TB + j):64 * (o * TB + j) + 64] for j in range(TB) for o in range(2)], 1)
         d = cols_through(m[0:B if lone else 128], d)
         for k in range(2 * TB):
             at = (t * 2 * TB + k) * PITCH
             z_ref[at:at + 64, :] = d[:, 128 * k:128 * k + 128]
 
+    staggered(pairs // TB, (moved, density, first_forward))
+
     lev = lev_ref[...]
     if lone:
         lev = jnp.where(iota((32, 128), 1) < B, lev[:32], lev[32:])
     deep = 32 if lone else 64
     through = (lambda a, d: halves_through(m[a:a + 128, :128], d)) if lone else (lambda a, d: cols_through(m[a:a + 128], d))
-    for t in range(64 // TA):
+
+    def second_forward(t, _):
         parts = [z_ref[pl.ds(t * TA + k, deep, stride=PITCH), :] for k in range(TA)]
         d = through(256, jnp.concatenate(parts, 1))
         g = jnp.concatenate([1.0 / (lev + la_ref[t * TA + k:t * TA + k + 1, :]) for k in range(TA)], 1)
-        d = through(384, d * g)
+        return d * g
+
+    def second_back(t, d):
+        d = through(384, d)
         for k in range(TA):
             z_ref[pl.ds(t * TA + k, deep, stride=PITCH), :] = d[:, 128 * k:128 * k + 128]
 
+    staggered(64 // TA, (second_forward, second_back))
+
     stores = []
     target = stage_ref if last else out_ref
-    for t in range(pairs // TB):
+
+    def first_back(t, _):
         parts = [z_ref[(t * 2 * TB + k) * PITCH:(t * 2 * TB + k) * PITCH + 64, :] for k in range(2 * TB)]
-        d = cols_through(m[128:192 if lone else 256], jnp.concatenate(parts, 1))
+        return cols_through(m[128:192 if lone else 256], jnp.concatenate(parts, 1))
+
+    def last_back(t, d):
         d = jnp.concatenate([d[:, 128 * k:128 * k + 128] for k in range(2 * TB)], 0)
         d = rows_through(d, m[768:1024])
         for j in range(TB):
@@ -246,13 +272,15 @@
                 part = pl.ds(at, TB * 128)
                 stores.append(pltpu.make_async_copy(stage_ref.at[:, part], out_ref.at[:, part], sems.at[1 + len(stores)]))
                 stores[-1].start()
+
+    staggered(pairs // TB, (first_back, last_back))
     for store in stores:
         store.wait()
 
 
-def pair_call(made, x, n0, n1, acc, last=False, TB=16, TA=32):
+def pair_call(made, x, n0, n1, acc, last=False, TB=4, TA=8, LB=4):
     first, lone = acc is None, n1 is None
-    TB = min(TB, 8) if lone else TB
+    TB = min(TB, LB) if lone else TB
     vm = pl.BlockSpec(memory_space=pltpu.VMEM)
     hbm = pl.BlockSpec(memory_space=pl.ANY)
     args = [x] + ([] if first else [n0]) + ([] if lone else [n1]) + ([] if first else [acc])
@@ -268,6 +296,7 @@
         if first:
             refs.insert(3, None)
         pair_kernel(TB, TA, first, last, lone, *refs)
+
     return pl.pallas_call(
         body,
         out_shape=jax.ShapeDtypeStruct((B, B * B), f32) if last else OUT((B, B * B), f32),

time: 67.6 us -> 66.1 us (0.978)
  Pallas kernels: 25.6 us -> 23.5 us
    pallas_call x4, Pallas kernels: 23.3 us -> 21.2 us  [pair_call(): pl.pallas_call(body, out_shape=jax.ShapeDtypeStruct((B, B * B), f32) if l...]
  transfers between devices with their start and end apart: 6 -> 6, of which waited for: 1 -> 1; matrix products, arithmetic and copies ran while one was open for 1% -> 1% of each run, Pallas kernels for 30% -> 28%
where the time goes in v1:
time: 66.1 us; the launch traced here: 65.7 us
  starting transfers between devices  39.2 us (59%)
  Pallas kernels  23.5 us (36%)
  waiting for transfers between devices  1.89 us (3%)
  other arithmetic  0.72 us (1%)
    ppermute x6, starting transfers between devices, permute(): lax.ppermute(value, AXES, [(p, target(p) % count) for p in range(count)])  39.2 us
    pallas_call x4, Pallas kernels, pair_call(): pl.pallas_call(body, out_shape=jax.ShapeDtypeStruct((B, B * B), f32) if l...  21.2 us
    pallas_call x1, Pallas kernels, prepare(): pl.pallas_call(lambda *refs: prepare_kernel(calls, *refs), out_shape=outs...  2.3 us
    ppermute x6, waiting for transfers between devices, permute(): lax.ppermute(value, AXES, [(p, target(p) % count) for p in range(count)])  1.89 us
  transfers between devices with their start and end apart: 6, of which 1 were waited for; matrix products, arithmetic and copies ran while one was open for 1% of the time, Pallas kernels for 28%

profile of v1, /device:TPU:1, one launch (start us, length us, event | category | flops | bytes accessed | tf_op | source)
XLA Modules:
  0.0 65.7 jit_solution(1299788579920874080)
XLA Ops:
  0.0 0.0 copy-start.3
  0.0 8.9 %collective-permute-start.1 = (bf16[64,4096]{1,0:T(8,128)(2,1)}, bf16[64,4096]{1,0:T(8,128)(2,1)S(1)}, u32[]{:S(2)}, u32[]{:S(2)}) collective-permute-start(bf16[64,4096]{1,0:T(8,128)(2,1)} %bitcast.4), channel_id=1, source_target_pairs={{0,1},{1,0},{2,3},{3,2},{4,5},{5,4},{6,7},{7,6},{8,9},{9,8},{10,11... | collective-permute-start | bytes 1572872 | tf_op jit(solution)/shard_map/ppermute | solution.py:317
  8.9 1.9 %collective-permute-start = (bf16[64,4096]{1,0:T(8,128)(2,1)}, bf16[64,4096]{1,0:T(8,128)(2,1)S(1)}, u32[]{:S(2)}, u32[]{:S(2)}) collective-permute-start(bf16[64,4096]{1,0:T(8,128)(2,1)} %bitcast.5), channel_id=1, source_target_pairs={{0,510},{1,3},{2,0},{3,5},{4,2},{5,7},{6,4},{7,9},{8,6},{9,11},{10... | collective-permute-start | bytes 1572872 | tf_op jit(solution)/shard_map/ppermute | solution.py:317
  10.8 0.7 %pad_add_fusion.refs_0_ = s32[6,512]{1,0:T(8,128)S(1)} fusion(s32[3,512]{1,0:T(4,128)} %bitcast.11, s32[3,512]{1,0:T(4,128)} %bitcast.12), kind=kLoop, calls=%fused_computation | loop fusion | flops 3072 | bytes 24576 | tf_op jit(solution)/shard_map/concatenate | solution.py:322
  11.5 0.0 copy-done.3
  11.5 0.0 copy-start
  11.5 0.0 copy-start.1
  11.6 0.0 copy-start.2
  11.6 2.3 %shard_map.64 = (bf16[1408,256]{1,0:T(8,128)(2,1)S(1)}, s32[2,8,128]{2,1,0:T(8,128)S(1)}, bf16[1408,256]{1,0:T(8,128)(2,1)S(1)}, s32[2,8,128]{2,1,0:T(8,128)S(1)...) custom-call(s32[6,512]{1,0:T(8,128)S(1)} %pad_add_fusion.refs_0_, ...), custom_call_target="tpu_custom_call" | custom-call | flops 3000000000 | bytes 1048576 | tf_op jit(solution)/shard_map/pallas_call | solution.py:151
  13.9 0.0 copy-done
  13.9 10.4 %collective-permute-start.3 = (bf16[64,4096]{1,0:T(8,128)(2,1)S(1)}, bf16[64,4096]{1,0:T(8,128)(2,1)S(1)}, u32[]{:S(2)}, u32[]{:S(2)}) collective-permute-start(bf16[64,4096]{1,0:T(8,128)(2,1)S(1)} %bitcast.6), channel_id=1, source_target_pairs={{0,2},{1,511},{2,4},{3,1},{4,6},{5,3},{6,8},{7,5},{8,10},{9,7},{10... | collective-permute-start | bytes 1572872 | tf_op jit(solution)/shard_map/ppermute | solution.py:317
  24.3 0.0 collective-permute-done.1.refs_1_
  24.3 0.0 copy-done.1
  24.3 0.0 copy-done.2
  24.4 5.3 %shard_map.65.refs_3_ = f32[64,4096]{1,0:T(8,128)S(1)} custom-call(bf16[64,4096]{1,0:T(8,128)(2,1)S(1)} %bitcast.7, bf16[64,4096]{1,0:T(8,128)(2,1)S(1)} %collective-permute-done.1.refs_1_, bf16[1408,256]{1,0:T(8,128)(2,1)S(1)} %get-tuple-element.18.refs_2_, s32[2,8,128]{2,1,0:T(8,128)S(1)} %get-tuple-element.19.refs_3_, f32[64,128]{1,0:T(8,128)S(1)} %copy-done.2, ...), custom_call_target="tpu_custom_call" | custom-call | flops 10000000000 | bytes 4194304 | tf_op jit(solution)/shard_map/pallas_call | solution.py:300
  29.7 1.9 %collective-permute-done.refs_1_ = bf16[64,4096]{1,0:T(8,128)(2,1)S(1)} collective-permute-done((bf16[64,4096]{1,0:T(8,128)(2,1)}, bf16[64,4096]{1,0:T(8,128)(2,1)S(1)}, u32[]{:S(2)}, u32[]{:S(2)}) %collective-permute-start) | collective-permute-done | bytes 524320 | tf_op jit(solution)/shard_map/ppermute | solution.py:317
  31.5 5.9 %collective-permute-start.5 = (bf16[64,4096]{1,0:T(8,128)(2,1)S(1)}, bf16[64,4096]{1,0:T(8,128)(2,1)S(1)}, u32[]{:S(2)}, u32[]{:S(2)}) collective-permute-start(bf16[64,4096]{1,0:T(8,128)(2,1)S(1)} %collective-permute-done.refs_1_), channel_id=1, source_target_pairs={{0,1},{1,0},{2,3},{3,2},{4,5},{5,4},{6,7},{7,6},{8,9},{9,8},{10,11... | collective-permute-start | bytes 1572872 | tf_op jit(solution)/shard_map/ppermute | solution.py:317
  37.5 1.9 %collective-permute-start.2 = (bf16[64,4096]{1,0:T(8,128)(2,1)S(1)}, bf16[64,4096]{1,0:T(8,128)(2,1)S(1)}, u32[]{:S(2)}, u32[]{:S(2)}) collective-permute-start(bf16[64,4096]{1,0:T(8,128)(2,1)S(1)} %collective-permute-done.refs_1_), channel_id=1, source_target_pairs={{0,511},{1,2},{2,1},{3,4},{4,3},{5,6},{6,5},{7,8},{8,7},{9,10},{10... | collective-permute-start | bytes 1572872 | tf_op jit(solution)/shard_map/ppermute | solution.py:317
  39.4 0.0 collective-permute-done.3.refs_1_
  39.4 10.1 %collective-permute-start.4 = (bf16[64,4096]{1,0:T(8,128)(2,1)S(1)}, bf16[64,4096]{1,0:T(8,128)(2,1)S(1)}, u32[]{:S(2)}, u32[]{:S(2)}) collective-permute-start(bf16[64,4096]{1,0:T(8,128)(2,1)S(1)} %collective-permute-done.3.refs_1_), channel_id=1, source_target_pairs={{0,1},{1,0},{2,3},{3,2},{4,5},{5,4},{6,7},{7,6},{8,9},{9,8},{10,11... | collective-permute-start | bytes 1572872 | tf_op jit(solution)/shard_map/ppermute | solution.py:317
  49.5 0.0 collective-permute-done.5.refs_2_
  49.6 5.5 %shard_map.66.refs_3_ = f32[64,4096]{1,0:T(8,128)S(1)} custom-call(bf16[64,4096]{1,0:T(8,128)(2,1)S(1)} %bitcast.8, bf16[64,4096]{1,0:T(8,128)(2,1)S(1)} %collective-permute-done.refs_1_, bf16[64,4096]{1,0:T(8,128)(2,1)S(1)} %collective-permute-done.5.refs_2_, f32[64,4096]{1,0:T(8,128)S(1)} %shard_map.65.refs_3_, ...), custom_call_target="tpu_custom_call" | custom-call | flops 10000000000 | bytes 4194304 | tf_op jit(solution)/shard_map/pallas_call | solution.py:300
  55.1 0.0 collective-permute-done.4.refs_2_
  55.1 5.5 %shard_map.67.refs_2_ = f32[64,4096]{1,0:T(8,128)S(1)} custom-call(bf16[64,4096]{1,0:T(8,128)(2,1)S(1)} %bitcast.9, bf16[64,4096]{1,0:T(8,128)(2,1)S(1)} %collective-permute-done.3.refs_1_, bf16[64,4096]{1,0:T(8,128)(2,1)S(1)} %collective-permute-done.4.refs_2_, f32[64,4096]{1,0:T(8,128)S(1)} %shard_map.66.refs_3_, ...), custom_call_target="tpu_custom_call" | custom-call | flops 10000000000 | bytes 4194304 | tf_op jit(solution)/shard_map/pallas_call | solution.py:300
  60.6 0.0 collective-permute-done.2.refs_1_
  60.6 4.9 %shard_map.68 = f32[64,4096]{1,0:T(8,128)} custom-call(bf16[64,4096]{1,0:T(8,128)(2,1)S(1)} %bitcast.10, bf16[64,4096]{1,0:T(8,128)(2,1)S(1)} %collective-permute-done.2.refs_1_, f32[64,4096]{1,0:T(8,128)S(1)} %shard_map.67.refs_2_, bf16[1408,256]{1,0:T(8,128)(2,1)S(1)} %get-tuple-element.27.refs_3_, s32[2,8,128]{2,1,0:T(8,128)S(1)} %get-tuple-element.28.refs_4_, ...), custom_call_target="tpu_custom_call" | custom-call | flops 10000000000 | bytes 4194304 | tf_op jit(solution)/shard_map/pallas_call | solution.py:300
Async XLA Ops:
  0.0 11.5 %copy-start.3 = (f32[64,128]{1,0:T(8,128)S(1)}, f32[64,128]{1,0:T(8,128)}, u32[]{:S(2)}) copy-start(f32[64,128]{1,0:T(8,128)} %constant.6.clone.refs_1_) | copy-start | bytes 98308
  0.0 24.3 %collective-permute-start.1 = (bf16[64,4096]{1,0:T(8,128)(2,1)}, bf16[64,4096]{1,0:T(8,128)(2,1)S(1)}, u32[]{:S(2)}, u32[]{:S(2)}) collective-permute-start(bf16[64,4096]{1,0:T(8,128)(2,1)} %bitcast.4), channel_id=1, source_target_pairs={{0,1},{1,0},{2,3},{3,2},{4,5},{5,4},{6,7},{7,6},{8,9},{9,8},{10,11... | collective-permute-start | bytes 1572872 | tf_op jit(solution)/shard_map/ppermute | solution.py:317
  8.9 22.7 %collective-permute-start = (bf16[64,4096]{1,0:T(8,128)(2,1)}, bf16[64,4096]{1,0:T(8,128)(2,1)S(1)}, u32[]{:S(2)}, u32[]{:S(2)}) collective-permute-start(bf16[64,4096]{1,0:T(8,128)(2,1)} %bitcast.5), channel_id=1, source_target_pairs={{0,510},{1,3},{2,0},{3,5},{4,2},{5,7},{6,4},{7,9},{8,6},{9,11},{10... | collective-permute-start | bytes 1572872 | tf_op jit(solution)/shard_map/ppermute | solution.py:317
  11.5 2.3 %copy-start = (bf16[1,64,4096]{2,1,0:T(8,128)(2,1)S(1)}, bf16[1,64,4096]{2,1,0:T(8,128)(2,1)}, u32[]{:S(2)}) copy-start(bf16[1,64,4096]{2,1,0:T(8,128)(2,1)} %param.6) | copy-start | bytes 1572868
  11.5 12.8 %copy-start.1 = (f32[64,128]{1,0:T(8,128)S(1)}, f32[64,128]{1,0:T(8,128)}, u32[]{:S(2)}) copy-start(f32[64,128]{1,0:T(8,128)} %constant.8.clone.refs_5_.refs_7_.refs_6_) | copy-start | bytes 98308
  11.6 12.8 %copy-start.2 = (f32[64,128]{1,0:T(8,128)S(1)}, f32[64,128]{1,0:T(8,128)}, u32[]{:S(2)}) copy-start(f32[64,128]{1,0:T(8,128)} %constant.7.clone.refs_4_.refs_6_.refs_5_) | copy-start | bytes 98308
  13.9 25.5 %collective-permute-start.3 = (bf16[64,4096]{1,0:T(8,128)(2,1)S(1)}, bf16[64,4096]{1,0:T(8,128)(2,1)S(1)}, u32[]{:S(2)}, u32[]{:S(2)}) collective-permute-start(bf16[64,4096]{1,0:T(8,128)(2,1)S(1)} %bitcast.6), channel_id=1, source_target_pairs={{0,2},{1,511},{2,4},{3,1},{4,6},{5,3},{6,8},{7,5},{8,10},{9,7},{10... | collective-permute-start | bytes 1572872 | tf_op jit(solution)/shard_map/ppermute | solution.py:317
  31.5 18.0 %collective-permute-start.5 = (bf16[64,4096]{1,0:T(8,128)(2,1)S(1)}, bf16[64,4096]{1,0:T(8,128)(2,1)S(1)}, u32[]{:S(2)}, u32[]{:S(2)}) collective-permute-start(bf16[64,4096]{1,0:T(8,128)(2,1)S(1)} %collective-permute-done.refs_1_), channel_id=1, source_target_pairs={{0,1},{1,0},{2,3},{3,2},{4,5},{5,4},{6,7},{7,6},{8,9},{9,8},{10,11... | collective-permute-start | bytes 1572872 | tf_op jit(solution)/shard_map/ppermute | solution.py:317
  37.5 23.2 %collective-permute-start.2 = (bf16[64,4096]{1,0:T(8,128)(2,1)S(1)}, bf16[64,4096]{1,0:T(8,128)(2,1)S(1)}, u32[]{:S(2)}, u32[]{:S(2)}) collective-permute-start(bf16[64,4096]{1,0:T(8,128)(2,1)S(1)} %collective-permute-done.refs_1_), channel_id=1, source_target_pairs={{0,511},{1,2},{2,1},{3,4},{4,3},{5,6},{6,5},{7,8},{8,7},{9,10},{10... | collective-permute-start | bytes 1572872 | tf_op jit(solution)/shard_map/ppermute | solution.py:317
  39.4 15.7 %collective-permute-start.4 = (bf16[64,4096]{1,0:T(8,128)(2,1)S(1)}, bf16[64,4096]{1,0:T(8,128)(2,1)S(1)}, u32[]{:S(2)}, u32[]{:S(2)}) collective-permute-start(bf16[64,4096]{1,0:T(8,128)(2,1)S(1)} %collective-permute-done.3.refs_1_), channel_id=1, source_target_pairs={{0,1},{1,0},{2,3},{3,2},{4,5},{5,4},{6,7},{7,6},{8,9},{9,8},{10,11... | collective-permute-start | bytes 1572872 | tf_op jit(solution)/shard_map/ppermute | solution.py:317

commit v2 on v1

--- a/solution.py
+++ b/solution.py
@@ -323,17 +323,18 @@
     swap = lambda p: p ^ 1
     near = permute(x, lambda p: p + 2 if p % 2 else p - 2)
     own = permute(x, swap)
-    made = prepare(tab, ((0, 1), (2, -1), (-2, 3), (-3, None)))
+    made = prepare(tab, ((0, 1), (2, None), (-1, -2), (3, -3)))
     later, mine = lax.optimization_barrier((x, made[0]))
     back = permute(later, lambda p: p - 2 if p % 2 else p + 2)
     acc = pair_call([mine, made[1]], x, x, own, None)
     near, acc = lax.optimization_barrier((near, acc))
+    far = permute(near, lambda p: p + 1 if p % 2 else p - 1)
     near_swap = permute(near, swap)
-    far = permute(near, lambda p: p + 1 if p % 2 else p - 1)
-    acc = pair_call(made[2:4], x, near, near_swap, acc)
+    acc = pair_call(made[2:4], x, near, None, acc)
+    back, acc = lax.optimization_barrier((back, acc))
     back_swap = permute(back, swap)
-    acc = pair_call(made[4:6], x, back, back_swap, acc)
-    acc = pair_call(made[6:8], x, far, None, acc, last=True)
+    acc = pair_call(made[4:6], x, near_swap, back, acc)
+    acc = pair_call(made[6:8], x, back_swap, far, acc, last=True)
     return acc.reshape(orbitals.shape)
 
 

time: 66.1 us -> 65.8 us (level)
  transfers between devices with their start and end apart: 6 -> 6, of which waited for: 1 -> 1; matrix products, arithmetic and copies ran while one was open for 1% -> 1% of each run, Pallas kernels for 28% -> 26%
where the time goes in v2:
time: 65.8 us; the launch traced here: 65.4 us
  starting transfers between devices  39.3 us (60%)
  Pallas kernels  23.3 us (35%)
  waiting for transfers between devices  1.67 us (3%)
  other arithmetic  0.72 us (1%)
    ppermute x6, starting transfers between devices, permute(): lax.ppermute(value, AXES, [(p, target(p) % count) for p in range(count)])  39.3 us
    pallas_call x4, Pallas kernels, pair_call(): pl.pallas_call(body, out_shape=jax.ShapeDtypeStruct((B, B * B), f32) if l...  20.9 us
    pallas_call x1, Pallas kernels, prepare(): pl.pallas_call(lambda *refs: prepare_kernel(calls, *refs), out_shape=outs...  2.42 us
    ppermute x6, waiting for transfers between devices, permute(): lax.ppermute(value, AXES, [(p, target(p) % count) for p in range(count)])  1.67 us
  transfers between devices with their start and end apart: 6, of which 1 were waited for; matrix products, arithmetic and copies ran while one was open for 1% of the time, Pallas kernels for 26%

profile of v2, /device:TPU:1, one launch (start us, length us, event | category | flops | bytes accessed | tf_op | source)
XLA Modules:
  0.0 65.4 jit_solution(15001441496226286357)
XLA Ops:
  0.0 0.0 copy-start.3
  0.0 8.9 %collective-permute-start.2 = (bf16[64,4096]{1,0:T(8,128)(2,1)}, bf16[64,4096]{1,0:T(8,128)(2,1)S(1)}, u32[]{:S(2)}, u32[]{:S(2)}) collective-permute-start(bf16[64,4096]{1,0:T(8,128)(2,1)} %bitcast.4), channel_id=1, source_target_pairs={{0,1},{1,0},{2,3},{3,2},{4,5},{5,4},{6,7},{7,6},{8,9},{9,8},{10,11... | collective-permute-start | bytes 1572872 | tf_op jit(solution)/shard_map/ppermute | solution.py:317
  8.9 1.9 %collective-permute-start.1 = (bf16[64,4096]{1,0:T(8,128)(2,1)}, bf16[64,4096]{1,0:T(8,128)(2,1)S(1)}, u32[]{:S(2)}, u32[]{:S(2)}) collective-permute-start(bf16[64,4096]{1,0:T(8,128)(2,1)} %bitcast.5), channel_id=1, source_target_pairs={{0,510},{1,3},{2,0},{3,5},{4,2},{5,7},{6,4},{7,9},{8,6},{9,11},{10... | collective-permute-start | bytes 1572872 | tf_op jit(solution)/shard_map/ppermute | solution.py:317
  10.8 0.7 %pad_add_fusion.refs_0_ = s32[6,512]{1,0:T(8,128)S(1)} fusion(s32[3,512]{1,0:T(4,128)} %bitcast.11, s32[3,512]{1,0:T(4,128)} %bitcast.12), kind=kLoop, calls=%fused_computation | loop fusion | flops 3072 | bytes 24576 | tf_op jit(solution)/shard_map/concatenate | solution.py:322
  11.5 0.0 copy-done.3
  11.5 0.0 copy-start
  11.5 0.0 copy-start.1
  11.6 0.0 copy-start.2
  11.6 2.4 %shard_map.64 = (bf16[1408,256]{1,0:T(8,128)(2,1)S(1)}, s32[2,8,128]{2,1,0:T(8,128)S(1)}, bf16[1408,256]{1,0:T(8,128)(2,1)S(1)}, s32[2,8,128]{2,1,0:T(8,128)S(1)...) custom-call(s32[6,512]{1,0:T(8,128)S(1)} %pad_add_fusion.refs_0_, ...), custom_call_target="tpu_custom_call" | custom-call | flops 3000000000 | bytes 1048576 | tf_op jit(solution)/shard_map/pallas_call | solution.py:151
  14.0 0.0 copy-done
  14.0 10.4 %collective-permute-start = (bf16[64,4096]{1,0:T(8,128)(2,1)S(1)}, bf16[64,4096]{1,0:T(8,128)(2,1)S(1)}, u32[]{:S(2)}, u32[]{:S(2)}) collective-permute-start(bf16[64,4096]{1,0:T(8,128)(2,1)S(1)} %bitcast.6), channel_id=1, source_target_pairs={{0,2},{1,511},{2,4},{3,1},{4,6},{5,3},{6,8},{7,5},{8,10},{9,7},{10... | collective-permute-start | bytes 1572872 | tf_op jit(solution)/shard_map/ppermute | solution.py:317
  24.4 0.0 collective-permute-done.2.refs_1_
  24.4 0.0 copy-done.1
  24.5 0.0 copy-done.2
  24.5 5.3 %shard_map.65.refs_2_ = f32[64,4096]{1,0:T(8,128)S(1)} custom-call(bf16[64,4096]{1,0:T(8,128)(2,1)S(1)} %bitcast.7, bf16[64,4096]{1,0:T(8,128)(2,1)S(1)} %collective-permute-done.2.refs_1_, bf16[1408,256]{1,0:T(8,128)(2,1)S(1)} %get-tuple-element.21.refs_2_, s32[2,8,128]{2,1,0:T(8,128)S(1)} %get-tuple-element.22.refs_3_, f32[64,128]{1,0:T(8,128)S(1)} %copy-done.2, ...), custom_call_target="tpu_custom_call" | custom-call | flops 10000000000 | bytes 4194304 | tf_op jit(solution)/shard_map/pallas_call | solution.py:300
  29.8 1.7 %collective-permute-done.1.refs_1_ = bf16[64,4096]{1,0:T(8,128)(2,1)S(1)} collective-permute-done((bf16[64,4096]{1,0:T(8,128)(2,1)}, bf16[64,4096]{1,0:T(8,128)(2,1)S(1)}, u32[]{:S(2)}, u32[]{:S(2)}) %collective-permute-start.1) | collective-permute-done | bytes 524320 | tf_op jit(solution)/shard_map/ppermute | solution.py:317
  31.4 6.1 %collective-permute-start.5 = (bf16[64,4096]{1,0:T(8,128)(2,1)S(1)}, bf16[64,4096]{1,0:T(8,128)(2,1)S(1)}, u32[]{:S(2)}, u32[]{:S(2)}) collective-permute-start(bf16[64,4096]{1,0:T(8,128)(2,1)S(1)} %collective-permute-done.1.refs_1_), channel_id=1, source_target_pairs={{0,1},{1,0},{2,3},{3,2},{4,5},{5,4},{6,7},{7,6},{8,9},{9,8},{10,11... | collective-permute-start | bytes 1572872 | tf_op jit(solution)/shard_map/ppermute | solution.py:317
  37.5 1.9 %collective-permute-start.4 = (bf16[64,4096]{1,0:T(8,128)(2,1)S(1)}, bf16[64,4096]{1,0:T(8,128)(2,1)S(1)}, u32[]{:S(2)}, u32[]{:S(2)}) collective-permute-start(bf16[64,4096]{1,0:T(8,128)(2,1)S(1)} %collective-permute-done.1.refs_1_), channel_id=1, source_target_pairs={{0,511},{1,2},{2,1},{3,4},{4,3},{5,6},{6,5},{7,8},{8,7},{9,10},{10... | collective-permute-start | bytes 1572872 | tf_op jit(solution)/shard_map/ppermute | solution.py:317
  39.4 3.9 %shard_map.66.refs_3_ = f32[64,4096]{1,0:T(8,128)S(1)} custom-call(bf16[64,4096]{1,0:T(8,128)(2,1)S(1)} %bitcast.8, bf16[64,4096]{1,0:T(8,128)(2,1)S(1)} %collective-permute-done.1.refs_1_, f32[64,4096]{1,0:T(8,128)S(1)} %shard_map.65.refs_2_, bf16[1408,256]{1,0:T(8,128)(2,1)S(1)} %get-tuple-element.25.refs_3_, s32[2,8,128]{2,1,0:T(8,128)S(1)} %get-tuple-element.26.refs_4_, ...), custom_call_target="tpu_custom_call" | custom-call | flops 10000000000 | bytes 4194304 | tf_op jit(solution)/shard_map/pallas_call | solution.py:300
  43.3 0.0 collective-permute-done.refs_2_
  43.3 10.1 %collective-permute-start.3 = (bf16[64,4096]{1,0:T(8,128)(2,1)S(1)}, bf16[64,4096]{1,0:T(8,128)(2,1)S(1)}, u32[]{:S(2)}, u32[]{:S(2)}) collective-permute-start(bf16[64,4096]{1,0:T(8,128)(2,1)S(1)} %collective-permute-done.refs_2_), channel_id=1, source_target_pairs={{0,1},{1,0},{2,3},{3,2},{4,5},{5,4},{6,7},{7,6},{8,9},{9,8},{10,11... | collective-permute-start | bytes 1572872 | tf_op jit(solution)/shard_map/ppermute | solution.py:317
  53.4 0.0 collective-permute-done.5.refs_1_
  53.5 5.5 %shard_map.67.refs_3_ = f32[64,4096]{1,0:T(8,128)S(1)} custom-call(bf16[64,4096]{1,0:T(8,128)(2,1)S(1)} %bitcast.9, bf16[64,4096]{1,0:T(8,128)(2,1)S(1)} %collective-permute-done.5.refs_1_, bf16[64,4096]{1,0:T(8,128)(2,1)S(1)} %collective-permute-done.refs_2_, f32[64,4096]{1,0:T(8,128)S(1)} %shard_map.66.refs_3_, ...), custom_call_target="tpu_custom_call" | custom-call | flops 10000000000 | bytes 4194304 | tf_op jit(solution)/shard_map/pallas_call | solution.py:300
  59.0 0.0 collective-permute-done.4.refs_2_
  59.0 0.0 collective-permute-done.3.refs_1_
  59.0 6.2 %shard_map.68 = f32[64,4096]{1,0:T(8,128)} custom-call(bf16[64,4096]{1,0:T(8,128)(2,1)S(1)} %bitcast.10, bf16[64,4096]{1,0:T(8,128)(2,1)S(1)} %collective-permute-done.3.refs_1_, bf16[64,4096]{1,0:T(8,128)(2,1)S(1)} %collective-permute-done.4.refs_2_, f32[64,4096]{1,0:T(8,128)S(1)} %shard_map.67.refs_3_, bf16[1408,256]{1,0:T(8,128)(2,1)S(1)} %get-tuple-element.31.refs_4_, ...), custom_call_target="tpu_custom_call" | custom-call | flops 10000000000 | bytes 4194304 | tf_op jit(solution)/shard_map/pallas_call | solution.py:300
Async XLA Ops:
  0.0 11.5 %copy-start.3 = (f32[64,128]{1,0:T(8,128)S(1)}, f32[64,128]{1,0:T(8,128)}, u32[]{:S(2)}) copy-start(f32[64,128]{1,0:T(8,128)} %constant.6.clone.refs_1_) | copy-start | bytes 98308
  0.0 24.4 %collective-permute-start.2 = (bf16[64,4096]{1,0:T(8,128)(2,1)}, bf16[64,4096]{1,0:T(8,128)(2,1)S(1)}, u32[]{:S(2)}, u32[]{:S(2)}) collective-permute-start(bf16[64,4096]{1,0:T(8,128)(2,1)} %bitcast.4), channel_id=1, source_target_pairs={{0,1},{1,0},{2,3},{3,2},{4,5},{5,4},{6,7},{7,6},{8,9},{9,8},{10,11... | collective-permute-start | bytes 1572872 | tf_op jit(solution)/shard_map/ppermute | solution.py:317
  8.9 22.5 %collective-permute-start.1 = (bf16[64,4096]{1,0:T(8,128)(2,1)}, bf16[64,4096]{1,0:T(8,128)(2,1)S(1)}, u32[]{:S(2)}, u32[]{:S(2)}) collective-permute-start(bf16[64,4096]{1,0:T(8,128)(2,1)} %bitcast.5), channel_id=1, source_target_pairs={{0,510},{1,3},{2,0},{3,5},{4,2},{5,7},{6,4},{7,9},{8,6},{9,11},{10... | collective-permute-start | bytes 1572872 | tf_op jit(solution)/shard_map/ppermute | solution.py:317
  11.5 2.5 %copy-start = (bf16[1,64,4096]{2,1,0:T(8,128)(2,1)S(1)}, bf16[1,64,4096]{2,1,0:T(8,128)(2,1)}, u32[]{:S(2)}) copy-start(bf16[1,64,4096]{2,1,0:T(8,128)(2,1)} %param.6) | copy-start | bytes 1572868
  11.5 12.9 %copy-start.1 = (f32[64,128]{1,0:T(8,128)S(1)}, f32[64,128]{1,0:T(8,128)}, u32[]{:S(2)}) copy-start(f32[64,128]{1,0:T(8,128)} %constant.8.clone.refs_5_.refs_6_.refs_7_) | copy-start | bytes 98308
  11.6 12.9 %copy-start.2 = (f32[64,128]{1,0:T(8,128)S(1)}, f32[64,128]{1,0:T(8,128)}, u32[]{:S(2)}) copy-start(f32[64,128]{1,0:T(8,128)} %constant.7.clone.refs_4_.refs_5_.refs_6_) | copy-start | bytes 98308
  14.0 29.3 %collective-permute-start = (bf16[64,4096]{1,0:T(8,128)(2,1)S(1)}, bf16[64,4096]{1,0:T(8,128)(2,1)S(1)}, u32[]{:S(2)}, u32[]{:S(2)}) collective-permute-start(bf16[64,4096]{1,0:T(8,128)(2,1)S(1)} %bitcast.6), channel_id=1, source_target_pairs={{0,2},{1,511},{2,4},{3,1},{4,6},{5,3},{6,8},{7,5},{8,10},{9,7},{10... | collective-permute-start | bytes 1572872 | tf_op jit(solution)/shard_map/ppermute | solution.py:317
  31.4 22.0 %collective-permute-start.5 = (bf16[64,4096]{1,0:T(8,128)(2,1)S(1)}, bf16[64,4096]{1,0:T(8,128)(2,1)S(1)}, u32[]{:S(2)}, u32[]{:S(2)}) collective-permute-start(bf16[64,4096]{1,0:T(8,128)(2,1)S(1)} %collective-permute-done.1.refs_1_), channel_id=1, source_target_pairs={{0,1},{1,0},{2,3},{3,2},{4,5},{5,4},{6,7},{7,6},{8,9},{9,8},{10,11... | collective-permute-start | bytes 1572872 | tf_op jit(solution)/shard_map/ppermute | solution.py:317
  37.5 21.5 %collective-permute-start.4 = (bf16[64,4096]{1,0:T(8,128)(2,1)S(1)}, bf16[64,4096]{1,0:T(8,128)(2,1)S(1)}, u32[]{:S(2)}, u32[]{:S(2)}) collective-permute-start(bf16[64,4096]{1,0:T(8,128)(2,1)S(1)} %collective-permute-done.1.refs_1_), channel_id=1, source_target_pairs={{0,511},{1,2},{2,1},{3,4},{4,3},{5,6},{6,5},{7,8},{8,7},{9,10},{10... | collective-permute-start | bytes 1572872 | tf_op jit(solution)/shard_map/ppermute | solution.py:317
  43.3 15.7 %collective-permute-start.3 = (bf16[64,4096]{1,0:T(8,128)(2,1)S(1)}, bf16[64,4096]{1,0:T(8,128)(2,1)S(1)}, u32[]{:S(2)}, u32[]{:S(2)}) collective-permute-start(bf16[64,4096]{1,0:T(8,128)(2,1)S(1)} %collective-permute-done.refs_2_), channel_id=1, source_target_pairs={{0,1},{1,0},{2,3},{3,2},{4,5},{5,4},{6,7},{7,6},{8,9},{9,8},{10,11... | collective-permute-start | bytes 1572872 | tf_op jit(solution)/shard_map/ppermute | solution.py:317

commit v3 on v2

--- a/solution.py
+++ b/solution.py
@@ -323,17 +323,17 @@
     swap = lambda p: p ^ 1
     near = permute(x, lambda p: p + 2 if p % 2 else p - 2)
     own = permute(x, swap)
-    made = prepare(tab, ((0, 1), (2, None), (-1, -2), (3, -3)))
+    made = prepare(tab, ((0, 1), (2, -1), (-2, None), (3, -3)))
     later, mine = lax.optimization_barrier((x, made[0]))
     back = permute(later, lambda p: p - 2 if p % 2 else p + 2)
     acc = pair_call([mine, made[1]], x, x, own, None)
     near, acc = lax.optimization_barrier((near, acc))
     far = permute(near, lambda p: p + 1 if p % 2 else p - 1)
     near_swap = permute(near, swap)
-    acc = pair_call(made[2:4], x, near, None, acc)
+    acc = pair_call(made[2:4], x, near, near_swap, acc)
     back, acc = lax.optimization_barrier((back, acc))
     back_swap = permute(back, swap)
-    acc = pair_call(made[4:6], x, near_swap, back, acc)
+    acc = pair_call(made[4:6], x, back, None, acc)
     acc = pair_call(made[6:8], x, back_swap, far, acc, last=True)
     return acc.reshape(orbitals.shape)
 

time: 65.8 us -> 69.5 us (1.056)
  waiting for transfers between devices: 1.67 us -> 18 us
  starting transfers between devices: 39.3 us -> 26.7 us
    ppermute x6, waiting for transfers between devices: 1.67 us -> 18 us  [permute(): lax.ppermute(value, AXES, [(p, target(p) % count) for p in range(count)])]
    ppermute x6, starting transfers between devices: 39.3 us -> 26.7 us  [permute(): lax.ppermute(value, AXES, [(p, target(p) % count) for p in range(count)])]
  transfers between devices with their start and end apart: 6 -> 6, of which waited for: 1 -> 2; matrix products, arithmetic and copies ran while one was open for 1% -> 1% of each run, Pallas kernels for 26% -> 25%
where the time goes in v3:
time: 69.5 us; the launch traced here: 69.1 us
  starting transfers between devices  26.7 us (38%)
  Pallas kernels  23.3 us (34%)
  waiting for transfers between devices  18 us (26%)
  other arithmetic  0.72 us (1%)
    ppermute x6, starting transfers between devices, permute(): lax.ppermute(value, AXES, [(p, target(p) % count) for p in range(count)])  26.7 us
    pallas_call x4, Pallas kernels, pair_call(): pl.pallas_call(body, out_shape=jax.ShapeDtypeStruct((B, B * B), f32) if l...  20.9 us
    ppermute x6, waiting for transfers between devices, permute(): lax.ppermute(value, AXES, [(p, target(p) % count) for p in range(count)])  18 us
    pallas_call x1, Pallas kernels, prepare(): pl.pallas_call(lambda *refs: prepare_kernel(calls, *refs), out_shape=outs...  2.42 us
  transfers between devices with their start and end apart: 6, of which 2 were waited for; matrix products, arithmetic and copies ran while one was open for 1% of the time, Pallas kernels for 25%

profile of v3, /device:TPU:1, one launch (start us, length us, event | category | flops | bytes accessed | tf_op | source)
XLA Modules:
  0.0 69.1 jit_solution(7286052527841349863)
XLA Ops:
  0.0 0.0 copy-start.3
  0.0 8.9 %collective-permute-start.2 = (bf16[64,4096]{1,0:T(8,128)(2,1)}, bf16[64,4096]{1,0:T(8,128)(2,1)S(1)}, u32[]{:S(2)}, u32[]{:S(2)}) collective-permute-start(bf16[64,4096]{1,0:T(8,128)(2,1)} %bitcast.4), channel_id=1, source_target_pairs={{0,1},{1,0},{2,3},{3,2},{4,5},{5,4},{6,7},{7,6},{8,9},{9,8},{10,11... | collective-permute-start | bytes 1572872 | tf_op jit(solution)/shard_map/ppermute | solution.py:317
  8.9 1.9 %collective-permute-start.1 = (bf16[64,4096]{1,0:T(8,128)(2,1)}, bf16[64,4096]{1,0:T(8,128)(2,1)S(1)}, u32[]{:S(2)}, u32[]{:S(2)}) collective-permute-start(bf16[64,4096]{1,0:T(8,128)(2,1)} %bitcast.5), channel_id=1, source_target_pairs={{0,510},{1,3},{2,0},{3,5},{4,2},{5,7},{6,4},{7,9},{8,6},{9,11},{10... | collective-permute-start | bytes 1572872 | tf_op jit(solution)/shard_map/ppermute | solution.py:317
  10.8 0.7 %pad_add_fusion.refs_0_ = s32[6,512]{1,0:T(8,128)S(1)} fusion(s32[3,512]{1,0:T(4,128)} %bitcast.11, s32[3,512]{1,0:T(4,128)} %bitcast.12), kind=kLoop, calls=%fused_computation | loop fusion | flops 3072 | bytes 24576 | tf_op jit(solution)/shard_map/concatenate | solution.py:322
  11.5 0.0 copy-done.3
  11.5 0.0 copy-start
  11.5 0.0 copy-start.1
  11.6 0.0 copy-start.2
  11.6 2.4 %shard_map.64 = (bf16[1408,256]{1,0:T(8,128)(2,1)S(1)}, s32[2,8,128]{2,1,0:T(8,128)S(1)}, bf16[1408,256]{1,0:T(8,128)(2,1)S(1)}, s32[2,8,128]{2,1,0:T(8,128)S(1)...) custom-call(s32[6,512]{1,0:T(8,128)S(1)} %pad_add_fusion.refs_0_, ...), custom_call_target="tpu_custom_call" | custom-call | flops 3000000000 | bytes 1048576 | tf_op jit(solution)/shard_map/pallas_call | solution.py:151
  14.0 0.0 collective-permute-done.2.refs_1_
  14.0 0.0 copy-done
  14.0 0.0 copy-done.1
  14.0 0.0 copy-done.2
  14.0 5.3 %shard_map.65.refs_3_ = f32[64,4096]{1,0:T(8,128)S(1)} custom-call(bf16[64,4096]{1,0:T(8,128)(2,1)S(1)} %bitcast.6, bf16[64,4096]{1,0:T(8,128)(2,1)S(1)} %collective-permute-done.2.refs_1_, bf16[1408,256]{1,0:T(8,128)(2,1)S(1)} %get-tuple-element.21.refs_2_, s32[2,8,128]{2,1,0:T(8,128)S(1)} %get-tuple-element.22.refs_3_, f32[64,128]{1,0:T(8,128)S(1)} %copy-done.1, ...), custom_call_target="tpu_custom_call" | custom-call | flops 10000000000 | bytes 4194304 | tf_op jit(solution)/shard_map/pallas_call | solution.py:300
  19.3 6.7 %collective-permute-done.1.refs_1_ = bf16[64,4096]{1,0:T(8,128)(2,1)S(1)} collective-permute-done((bf16[64,4096]{1,0:T(8,128)(2,1)}, bf16[64,4096]{1,0:T(8,128)(2,1)S(1)}, u32[]{:S(2)}, u32[]{:S(2)}) %collective-permute-start.1) | collective-permute-done | bytes 524320 | tf_op jit(solution)/shard_map/ppermute | solution.py:317
  26.1 4.0 %collective-permute-start.3 = (bf16[64,4096]{1,0:T(8,128)(2,1)S(1)}, bf16[64,4096]{1,0:T(8,128)(2,1)S(1)}, u32[]{:S(2)}, u32[]{:S(2)}) collective-permute-start(bf16[64,4096]{1,0:T(8,128)(2,1)S(1)} %collective-permute-done.1.refs_1_), channel_id=1, source_target_pairs={{0,1},{1,0},{2,3},{3,2},{4,5},{5,4},{6,7},{7,6},{8,9},{9,8},{10,11... | collective-permute-start | bytes 1572872 | tf_op jit(solution)/shard_map/ppermute | solution.py:317
  30.1 7.9 %collective-permute-start = (bf16[64,4096]{1,0:T(8,128)(2,1)S(1)}, bf16[64,4096]{1,0:T(8,128)(2,1)S(1)}, u32[]{:S(2)}, u32[]{:S(2)}) collective-permute-start(bf16[64,4096]{1,0:T(8,128)(2,1)S(1)} %bitcast.7), channel_id=1, source_target_pairs={{0,2},{1,511},{2,4},{3,1},{4,6},{5,3},{6,8},{7,5},{8,10},{9,7},{10... | collective-permute-start | bytes 1572872 | tf_op jit(solution)/shard_map/ppermute | solution.py:317
  37.9 1.9 %collective-permute-start.5 = (bf16[64,4096]{1,0:T(8,128)(2,1)S(1)}, bf16[64,4096]{1,0:T(8,128)(2,1)S(1)}, u32[]{:S(2)}, u32[]{:S(2)}) collective-permute-start(bf16[64,4096]{1,0:T(8,128)(2,1)S(1)} %collective-permute-done.1.refs_1_), channel_id=1, source_target_pairs={{0,511},{1,2},{2,1},{3,4},{4,3},{5,6},{6,5},{7,8},{8,7},{9,10},{10... | collective-permute-start | bytes 1572872 | tf_op jit(solution)/shard_map/ppermute | solution.py:317
  39.9 0.0 collective-permute-done.3.refs_2_
  39.9 5.5 %shard_map.66.refs_2_ = f32[64,4096]{1,0:T(8,128)S(1)} custom-call(bf16[64,4096]{1,0:T(8,128)(2,1)S(1)} %bitcast.8, bf16[64,4096]{1,0:T(8,128)(2,1)S(1)} %collective-permute-done.1.refs_1_, bf16[64,4096]{1,0:T(8,128)(2,1)S(1)} %collective-permute-done.3.refs_2_, f32[64,4096]{1,0:T(8,128)S(1)} %shard_map.65.refs_3_, ...), custom_call_target="tpu_custom_call" | custom-call | flops 10000000000 | bytes 4194304 | tf_op jit(solution)/shard_map/pallas_call | solution.py:300
  45.4 11.3 %collective-permute-done.refs_1_ = bf16[64,4096]{1,0:T(8,128)(2,1)S(1)} collective-permute-done((bf16[64,4096]{1,0:T(8,128)(2,1)S(1)}, bf16[64,4096]{1,0:T(8,128)(2,1)S(1)}, u32[]{:S(2)}, u32[]{:S(2)}) %collective-permute-start) | collective-permute-done | bytes 524320 | tf_op jit(solution)/shard_map/ppermute | solution.py:317
  56.7 2.1 %collective-permute-start.4 = (bf16[64,4096]{1,0:T(8,128)(2,1)S(1)}, bf16[64,4096]{1,0:T(8,128)(2,1)S(1)}, u32[]{:S(2)}, u32[]{:S(2)}) collective-permute-start(bf16[64,4096]{1,0:T(8,128)(2,1)S(1)} %collective-permute-done.refs_1_), channel_id=1, source_target_pairs={{0,1},{1,0},{2,3},{3,2},{4,5},{5,4},{6,7},{7,6},{8,9},{9,8},{10,11... | collective-permute-start | bytes 1572872 | tf_op jit(solution)/shard_map/ppermute | solution.py:317
  58.8 3.9 %shard_map.67.refs_3_ = f32[64,4096]{1,0:T(8,128)S(1)} custom-call(bf16[64,4096]{1,0:T(8,128)(2,1)S(1)} %bitcast.9, bf16[64,4096]{1,0:T(8,128)(2,1)S(1)} %collective-permute-done.refs_1_, f32[64,4096]{1,0:T(8,128)S(1)} %shard_map.66.refs_2_, bf16[1408,256]{1,0:T(8,128)(2,1)S(1)} %get-tuple-element.29.refs_3_, s32[2,8,128]{2,1,0:T(8,128)S(1)} %get-tuple-element.30.refs_4_, ...), custom_call_target="tpu_custom_call" | custom-call | flops 10000000000 | bytes 4194304 | tf_op jit(solution)/shard_map/pallas_call | solution.py:300
  62.7 0.0 collective-permute-done.5.refs_2_
  62.7 0.0 collective-permute-done.4.refs_1_
  62.7 6.2 %shard_map.68 = f32[64,4096]{1,0:T(8,128)} custom-call(bf16[64,4096]{1,0:T(8,128)(2,1)S(1)} %bitcast.10, bf16[64,4096]{1,0:T(8,128)(2,1)S(1)} %collective-permute-done.4.refs_1_, bf16[64,4096]{1,0:T(8,128)(2,1)S(1)} %collective-permute-done.5.refs_2_, f32[64,4096]{1,0:T(8,128)S(1)} %shard_map.67.refs_3_, bf16[1408,256]{1,0:T(8,128)(2,1)S(1)} %get-tuple-element.31.refs_4_, ...), custom_call_target="tpu_custom_call" | custom-call | flops 10000000000 | bytes 4194304 | tf_op jit(solution)/shard_map/pallas_call | solution.py:300
Async XLA Ops:
  0.0 11.5 %copy-start.3 = (f32[64,128]{1,0:T(8,128)S(1)}, f32[64,128]{1,0:T(8,128)}, u32[]{:S(2)}) copy-start(f32[64,128]{1,0:T(8,128)} %constant.6.clone.refs_1_) | copy-start | bytes 98308
  0.0 14.0 %collective-permute-start.2 = (bf16[64,4096]{1,0:T(8,128)(2,1)}, bf16[64,4096]{1,0:T(8,128)(2,1)S(1)}, u32[]{:S(2)}, u32[]{:S(2)}) collective-permute-start(bf16[64,4096]{1,0:T(8,128)(2,1)} %bitcast.4), channel_id=1, source_target_pairs={{0,1},{1,0},{2,3},{3,2},{4,5},{5,4},{6,7},{7,6},{8,9},{9,8},{10,11... | collective-permute-start | bytes 1572872 | tf_op jit(solution)/shard_map/ppermute | solution.py:317
  8.9 17.2 %collective-permute-start.1 = (bf16[64,4096]{1,0:T(8,128)(2,1)}, bf16[64,4096]{1,0:T(8,128)(2,1)S(1)}, u32[]{:S(2)}, u32[]{:S(2)}) collective-permute-start(bf16[64,4096]{1,0:T(8,128)(2,1)} %bitcast.5), channel_id=1, source_target_pairs={{0,510},{1,3},{2,0},{3,5},{4,2},{5,7},{6,4},{7,9},{8,6},{9,11},{10... | collective-permute-start | bytes 1572872 | tf_op jit(solution)/shard_map/ppermute | solution.py:317
  11.5 2.5 %copy-start = (bf16[1,64,4096]{2,1,0:T(8,128)(2,1)S(1)}, bf16[1,64,4096]{2,1,0:T(8,128)(2,1)}, u32[]{:S(2)}) copy-start(bf16[1,64,4096]{2,1,0:T(8,128)(2,1)} %param.6) | copy-start | bytes 1572868
  11.5 2.5 %copy-start.1 = (f32[64,128]{1,0:T(8,128)S(1)}, f32[64,128]{1,0:T(8,128)}, u32[]{:S(2)}) copy-start(f32[64,128]{1,0:T(8,128)} %constant.7.clone.refs_4_.refs_6_.refs_5_) | copy-start | bytes 98308
  11.6 2.5 %copy-start.2 = (f32[64,128]{1,0:T(8,128)S(1)}, f32[64,128]{1,0:T(8,128)}, u32[]{:S(2)}) copy-start(f32[64,128]{1,0:T(8,128)} %constant.8.clone.refs_5_.refs_7_.refs_6_) | copy-start | bytes 98308
  26.1 13.8 %collective-permute-start.3 = (bf16[64,4096]{1,0:T(8,128)(2,1)S(1)}, bf16[64,4096]{1,0:T(8,128)(2,1)S(1)}, u32[]{:S(2)}, u32[]{:S(2)}) collective-permute-start(bf16[64,4096]{1,0:T(8,128)(2,1)S(1)} %collective-permute-done.1.refs_1_), channel_id=1, source_target_pairs={{0,1},{1,0},{2,3},{3,2},{4,5},{5,4},{6,7},{7,6},{8,9},{9,8},{10,11... | collective-permute-start | bytes 1572872 | tf_op jit(solution)/shard_map/ppermute | solution.py:317
  30.1 26.6 %collective-permute-start = (bf16[64,4096]{1,0:T(8,128)(2,1)S(1)}, bf16[64,4096]{1,0:T(8,128)(2,1)S(1)}, u32[]{:S(2)}, u32[]{:S(2)}) collective-permute-start(bf16[64,4096]{1,0:T(8,128)(2,1)S(1)} %bitcast.7), channel_id=1, source_target_pairs={{0,2},{1,511},{2,4},{3,1},{4,6},{5,3},{6,8},{7,5},{8,10},{9,7},{10... | collective-permute-start | bytes 1572872 | tf_op jit(solution)/shard_map/ppermute | solution.py:317
  37.9 24.8 %collective-permute-start.5 = (bf16[64,4096]{1,0:T(8,128)(2,1)S(1)}, bf16[64,4096]{1,0:T(8,128)(2,1)S(1)}, u32[]{:S(2)}, u32[]{:S(2)}) collective-permute-start(bf16[64,4096]{1,0:T(8,128)(2,1)S(1)} %collective-permute-done.1.refs_1_), channel_id=1, source_target_pairs={{0,511},{1,2},{2,1},{3,4},{4,3},{5,6},{6,5},{7,8},{8,7},{9,10},{10... | collective-permute-start | bytes 1572872 | tf_op jit(solution)/shard_map/ppermute | solution.py:317
  56.7 6.0 %collective-permute-start.4 = (bf16[64,4096]{1,0:T(8,128)(2,1)S(1)}, bf16[64,4096]{1,0:T(8,128)(2,1)S(1)}, u32[]{:S(2)}, u32[]{:S(2)}) collective-permute-start(bf16[64,4096]{1,0:T(8,128)(2,1)S(1)} %collective-permute-done.refs_1_), channel_id=1, source_target_pairs={{0,1},{1,0},{2,3},{3,2},{4,5},{5,4},{6,7},{7,6},{8,9},{9,8},{10,11... | collective-permute-start | bytes 1572872 | tf_op jit(solution)/shard_map/ppermute | solution.py:317
